TPU v7x, 32 devices: a whole 2x2x4 slice. The times are simulated.
32 devices in a mesh: gx: 8 (over y, x, core), yz: 4 (over z).
Axes of the slice: x: 2, y: 2, z: 4, core: 2. Of those that a mesh axis runs over, the one named last changes fastest.
Arguments:
- spectra: bfloat16 [2, 20, 640, 16, 512], P(None, None, None, 'gx', 'yz'), may hold values from -6 to 6
- kernel_mesh: float32 [20], replicated, may hold values from 0.02 to 6, as said below
- density: float32 [640, 16, 512], P('gx', None, 'yz'), may hold values from 0.05 to 1
- local_wave: float32 [640, 16, 512], P('gx', None, 'yz'), may hold values from 0.15 to 4.8
- wave_density: float32 [640, 16, 512], P('gx', None, 'yz'), may hold values from -1.2 to 1.2
- wave_gradient: float32 [3, 640, 16, 512], P(None, 'gx', None, 'yz'), may hold values from -0.6 to 0.6
Outputs:
- potential: float32 [640, 16, 512], P('gx', None, 'yz')
Inputs may be any that keep to these rules, and one draw needn't show every extreme that they name: `kernel_mesh`: strictly increasing; entry 0 is at most 0.1 and entry 19 at least 5.0.
All inputs are finite; a program needn't handle non-finite values.
Results may differ from a plain program's by a relative error of at most 0.0033.
Values sent between devices are 32-bit elements.
A program may use at most 192 MiB of HBM per device.

v0:
```python
import math
import jax
import jax.numpy as jnp
from jax import lax
from jax.sharding import PartitionSpec as P


def extended(block, sides, width):
    for axis, dim in sides:
        count = lax.axis_size(axis)
        forward = [(i, i + 1) for i in range(count - 1)]
        forward.append((count - 1, 0))
        backward = [(target, source) for source, target in forward]
        low = lax.ppermute(
            lax.slice_in_dim(block, block.shape[dim] - width, None, axis=dim), axis, forward
        )
        high = lax.ppermute(lax.slice_in_dim(block, 0, width, axis=dim), axis, backward)
        block = jnp.concatenate([low, block, high], axis=dim)
    return block


def dft_tables(length):
    rows_index = lax.broadcasted_iota(jnp.int32, (length, length), 0)
    cols_index = lax.broadcasted_iota(jnp.int32, (length, length), 1)
    phases = rows_index * cols_index % length
    angles = phases.astype(jnp.float32) * (2.0 * math.pi / length)
    return jnp.stack([jnp.cos(angles), -jnp.sin(angles)]).astype(jnp.bfloat16)


def spline_second(kernel_mesh):
    points = kernel_mesh.shape[0]
    spacing = kernel_mesh[1:] - kernel_mesh[:-1]
    identity = jnp.eye(points, dtype=jnp.float32)
    right_side = (identity[2:] - identity[1:-1]) / spacing[1:, None] - (
        identity[1:-1] - identity[:-2]
    ) / spacing[:-1, None]
    zero_entry = jnp.zeros((1,), jnp.float32)
    lower_band = jnp.concatenate([zero_entry, spacing[1:-1] / 6.0])
    main_band = (spacing[:-1] + spacing[1:]) / 3.0
    upper_band = jnp.concatenate([spacing[1:-1] / 6.0, zero_entry])
    interior = lax.linalg.tridiagonal_solve(lower_band, main_band, upper_band, right_side)
    border = jnp.zeros((1, points), jnp.float32)
    return jnp.concatenate([border, interior, border])


def basis_terms(weight_a, weight_b, span_width, lower_hot, upper_hot, second_lower, second_upper):
    basis_value = (
        weight_a * lower_hot
        + weight_b * upper_hot
        + (weight_a * weight_a * weight_a - weight_a) * span_width * span_width / 6.0 * second_lower
        + (weight_b * weight_b * weight_b - weight_b) * span_width * span_width / 6.0 * second_upper
    )
    basis_slope = (
        (upper_hot - lower_hot) / span_width
        - (3.0 * weight_a * weight_a - 1.0) * span_width / 6.0 * second_lower
        + (3.0 * weight_b * weight_b - 1.0) * span_width / 6.0 * second_upper
    )
    return (basis_value, basis_slope)


def contract(components, local_wave, kernel_mesh, second):
    points = kernel_mesh.shape[0]
    interval = jnp.zeros(local_wave.shape, jnp.int32)
    for index in range(1, points - 1):
        interval = interval + (local_wave >= kernel_mesh[index]).astype(jnp.int32)
    labels = lax.broadcasted_iota(jnp.int32, (points, 1, 1, 1), 0)
    lower_hot = (labels == interval[None]).astype(jnp.float32)
    upper_hot = (labels == interval[None] + 1).astype(jnp.float32)
    column = kernel_mesh.reshape((points, 1, 1, 1))
    lower_point = jnp.sum(lower_hot * column, axis=0)
    finish_point = jnp.sum(upper_hot * column, axis=0)
    span_width = finish_point - lower_point
    weight_a = (finish_point - local_wave) / span_width
    weight_b = (local_wave - lower_point) / span_width
    second_lower = jnp.einsum("ba,bxyz->axyz", second, lower_hot, precision=lax.Precision.HIGHEST)
    second_upper = jnp.einsum("ba,bxyz->axyz", second, upper_hot, precision=lax.Precision.HIGHEST)
    basis_value, basis_slope = basis_terms(
        weight_a, weight_b, span_width, lower_hot, upper_hot, second_lower, second_upper
    )
    return (jnp.sum(components * basis_value, axis=0), jnp.sum(components * basis_slope, axis=0))


def shards(spectra, kernel_mesh, density, local_wave, wave_density, wave_gradient):
    length = spectra.shape[2]
    tables = dft_tables(length)
    accumulated = jnp.einsum("pckyz,pkx->cxyz", spectra, tables, preferred_element_type=jnp.float32)
    components = accumulated * length ** (-0.5)
    second = spline_second(kernel_mesh)
    slab_density, slab_wave, slab_rate = (
        lax.all_to_all(density, "gx", split_axis=1, concat_axis=0, tiled=True),
        lax.all_to_all(local_wave, "gx", split_axis=1, concat_axis=0, tiled=True),
        lax.all_to_all(wave_density, "gx", split_axis=1, concat_axis=0, tiled=True),
    )
    sum_value, sum_slope = contract(components, slab_wave, kernel_mesh, second)
    slab_local = sum_value + slab_density * slab_rate * sum_slope
    slab_scale = slab_density * sum_slope
    local_term, grad_scale = (
        lax.all_to_all(slab_local, "gx", split_axis=0, concat_axis=1, tiled=True),
        lax.all_to_all(slab_scale, "gx", split_axis=0, concat_axis=1, tiled=True),
    )
    flux_first = grad_scale * wave_gradient[0]
    flux_second = grad_scale * wave_gradient[1]
    flux_third = grad_scale * wave_gradient[2]
    padded_first = extended(flux_first, (("gx", 0),), 1)
    padded_third = extended(flux_third, (("yz", 2),), 1)
    divergence = 0.5 * (padded_first[2:] - padded_first[:-2])
    divergence = divergence + 0.5 * (jnp.roll(flux_second, -1, 1) - jnp.roll(flux_second, 1, 1))
    divergence = divergence + 0.5 * (padded_third[:, :, 2:] - padded_third[:, :, :-2])
    return local_term - divergence


def solution(mesh):
    return jax.shard_map(
        shards,
        mesh=mesh,
        in_specs=(
            P(None, None, None, "gx", "yz"),
            P(),
            P("gx", None, "yz"),
            P("gx", None, "yz"),
            P("gx", None, "yz"),
            P(None, "gx", None, "yz"),
        ),
        out_specs=P("gx", None, "yz"),
        check_vma=False,
    )
```

profile of v0, /device:TPU:0, one launch (start us, length us, event | category | flops | bytes accessed | tf_op | source)
XLA Modules:
  0.0 220.2 jit_solution(14158756007778748389)
XLA Ops:
  0.0 2.1 copy.69
  2.1 5.2 %all-to-all-start = ((f32[80,16,128]{2,0,1:T(8,128)}), f32[80,16,128]{2,0,1:T(8,128)S(1)}, u32[]{:S(2)}, u32[]{:S(2)}) async-start(f32[80,16,128]{2,0,1:T(8,128)} %copy.69), calls=%async_computation | async-start | bytes 1310720 | tf_op jit(solution)/shard_map/all_to_all | solution.py:91
  7.3 0.8 slice_subtract_fusion.19
  8.1 0.1 add_multiply_fusion
  8.3 0.7 fusion.83
  9.0 0.7 fusion.84
  40.5 0.1 fusion.37
  40.5 10.6 %fusion.43 = (f32[1,20]{1,0:T(1,128)S(1)}, f32[1,20]{1,0:T(1,128)S(1)}, f32[1,20]{1,0:T(1,128)S(1)}, f32[1,20]{1,0:T(1,128)S(1)}, f32[1,20]{1,0:T(1,128)S(1)}, /...) fusion(f32[18,20]{1,0:T(8,128)S(1)} %fusion.37, ...), kind=kLoop, calls=%fused_computation.98 | loop fusion | flops 980 | bytes 2852 | tf_op jit(solution)/shard_map/eval_jaxpr/div | solution.py:41
  52.5 2.2 copy.77
  54.6 2.1 copy.79
  57.4 0.7 multiply_subtract_fusion.2
  58.1 0.1 concatenate.26
  58.2 2.0 fusion.85
  60.2 7.7 %negate_convert_fusion = (bf16[1,640,640]{1,2,0:T(8,128)(2,1)}, bf16[1,640,640]{1,2,0:T(8,128)(2,1)}) fusion(), kind=kLoop, calls=%fused_computation.21 | loop fusion | flops 4915200 | bytes 1638400 | tf_op jit(solution)/shard_map/convert.1
  67.9 4.2 %all-to-all-start.1 = ((f32[80,16,128]{2,0,1:T(8,128)}), f32[80,16,128]{2,0,1:T(8,128)}, u32[]{:S(2)}, u32[]{:S(2)}) async-start(f32[80,16,128]{2,0,1:T(8,128)} %copy.77), calls=%async_computation.1 | async-start | bytes 1310720 | tf_op jit(solution)/shard_map/all_to_all | solution.py:90
  72.2 12.2 %broadcast_add_fusion = (s32[640,2,128]{2,0,1:T(8,128)S(1)}, s32[640,2,128]{2,0,1:T(8,128)S(1)}) fusion(f32[]{:T(128)} %bitcast.25, f32[]{:T(128)} %bitcast.24, f32[]{:T(128)} %bitcast.23, f32[]{:T(128)} %bitcast.22, f32[]{:T(128)} %bitcast.21, f32[]{:T(128)} %bitcast.20, f32[]{:T(128)} %bitcast.19, f32[]{:T(128)} %bitcast.18, f32[]{:T(128)} %bitcast.17, ...), kind=kLoop, calls=%fused_computation.85 | loop fusion | flops 8847360 | bytes 1966152 | tf_op jit(solution)/shard_map/add | solution.py:68
  84.4 3.5 %select_reduce_fusion = (f32[640,2,128]{2,0,1:T(8,128)S(1)}, f32[640,2,128]{2,0,1:T(8,128)S(1)}) fusion(f32[20]{0:T(128)} %param.7, s32[640,2,128]{2,0,1:T(8,128)S(1)} %get-tuple-element.50, s32[640,2,128]{2,0,1:T(8,128)S(1)} %get-tuple-element.49), kind=kLoop, calls=%fused_computation.11 | loop fusion | flops 19333120 | bytes 2621520 | tf_op jit(solution)/shard_map/reduce_sum | solution.py:70
  87.9 4.4 %iota_compare_fusion = (pred[20,640,2,128]{3,1,2,0:T(32,128)(4,1)S(1)}, pred[20,640,2,128]{3,1,2,0:T(32,128)(4,1)}) fusion(s32[640,2,128]{2,0,1:T(8,128)S(1)} %get-tuple-element.49, s32[640,2,128]{2,0,1:T(8,128)S(1)} %get-tuple-element.50), kind=kLoop, calls=%fused_computation.13 | loop fusion | flops 6553600 | bytes 7864320 | tf_op jit(solution)/shard_map/eq | solution.py:68
  92.4 1.2 fusion.19
  93.6 0.8 copy-done.2
  94.5 1.3 fusion.22
  95.7 4.4 %all-to-all-start.2 = ((f32[80,16,128]{2,0,1:T(8,128)}), f32[80,16,128]{2,0,1:T(8,128)}, u32[]{:S(2)}, u32[]{:S(2)}) async-start(f32[80,16,128]{2,0,1:T(8,128)} %copy.79), calls=%async_computation.2 | async-start | bytes 1310720 | tf_op jit(solution)/shard_map/all_to_all | solution.py:92
  100.1 2.0 copy.78
  102.1 17.0 %fusion.2 = f32[20,640,2,128]{3,0,2,1:T(8,128)} fusion(pred[20,640,2,128]{3,1,2,0:T(32,128)(4,1)} %get-tuple-element.126, f32[20,20]{1,0:T(8,128)S(1)} %concatenate.26), kind=kOutput, calls=%fused_computation.2 | convolution fusion | flops 786432000 | bytes 16385600 | tf_op jit(solution)/shard_map/ba,bxyz->axyz/dot_general | solution.py:75
  119.1 26.9 %fusion = f32[20,640,2,128]{3,0,2,1:T(8,128)} fusion(pred[20,640,2,128]{3,1,2,0:T(32,128)(4,1)S(1)} %get-tuple-element.125, f32[20,20]{1,0:T(8,128)S(1)} %concatenate.26), kind=kOutput, calls=%fused_computation | convolution fusion | flops 786432000 | bytes 16385600 | tf_op jit(solution)/shard_map/ba,bxyz->axyz/dot_general | solution.py:76
  146.1 1.1 copy.80
  147.2 1.8 fusion.15
  148.9 32.3 %fusion.4 = (f32[640,2,128]{2,0,1:T(8,128)S(1)}, f32[640,2,128]{2,0,1:T(8,128)}) fusion(f32[20,640,2,128]{3,0,2,1:T(8,128)} %fusion, f32[20,640,2,128]{3,0,2,1:T(8,128)} %fusion.2, f32[640,2,128]{2,0,1:T(8,128)S(1)} %get-tuple-element.68, f32[640,2,128]{2,0,1:T(8,128)S(1)} %get-tuple-element.67, f32[640,2,128]{2,0,1:T(8,128)} %get-tuple-element.13, ...), kind=kOutput, calls=%fused_computation.6 | convolution fusion | flops 8463646720 | bytes 48168960 | tf_op jit(solution)/shard_map/pckyz,pkx->cxyz/dot_general | solution.py:86
  181.2 1.2 fusion.33
  182.5 1.4 copy.86
  183.8 4.1 %all-to-all-start.4 = ((f32[640,2,128]{2,1,0:T(2,128)}), f32[640,2,128]{2,1,0:T(2,128)S(1)}, u32[]{:S(2)}, u32[]{:S(2)}) async-start(f32[640,2,128]{2,1,0:T(2,128)} %copy.86), calls=%async_computation.4 | async-start | bytes 1310720 | tf_op jit(solution)/shard_map/all_to_all | solution.py:99
  188.0 2.7 %fusion.78 = (f32[1,80,16,128]{3,2,1,0:T(8,128)S(1)}, f32[1,80,16,128]{3,2,1,0:T(8,128)}, f32[1,80,16,128]{3,2,1,0:T(8,128)}) fusion(f32[3,80,16,128]{3,2,1,0:T(8,128)} %param.11), kind=kLoop, calls=%fused_computation.151 | loop fusion | bytes 3932160 | tf_op jit(solution)/shard_map/slice | solution.py:102
  190.7 1.4 copy.83
  192.0 7.1 %all-to-all-done.4 = f32[640,2,128]{2,1,0:T(2,128)S(1)} async-done(((f32[640,2,128]{2,1,0:T(2,128)}), f32[640,2,128]{2,1,0:T(2,128)S(1)}, u32[]{:S(2)}, u32[]{:S(2)}) %all-to-all-start.4) | async-done | bytes 655392 | tf_op jit(solution)/shard_map/all_to_all | solution.py:99
  199.1 3.5 %all-to-all-start.3 = ((f32[640,2,128]{2,1,0:T(2,128)}), f32[640,2,128]{2,1,0:T(2,128)S(1)}, u32[]{:S(2)}, u32[]{:S(2)}) async-start(f32[640,2,128]{2,1,0:T(2,128)} %copy.83), calls=%async_computation.3 | async-start | bytes 1310720 | tf_op jit(solution)/shard_map/all_to_all | solution.py:98
  202.7 1.9 fusion.30
  204.7 1.0 fusion.82
  205.7 1.3 copy.92
  207.0 3.6 %collective-permute-start.2 = (f32[80,16,1]{0,1,2:T(8,128)S(1)}, f32[80,16,1]{0,1,2:T(8,128)S(1)}, u32[]{:S(2)}, u32[]{:S(2)}) collective-permute-start(f32[80,16,1]{0,1,2:T(8,128)S(1)} %copy.92), channel_id=1, source_target_pairs={{1,0},{2,1},{3,2},{0,3},{5,4},{6,5},{7,6},{4,7},{9,8},{10,9},{11,1... | collective-permute-start | bytes 15368 | tf_op jit(solution)/shard_map/ppermute | solution.py:17
  210.7 0.2 copy.94
  210.9 2.3 %collective-permute-start = (f32[1,16,128]{2,0,1:T(1,128)S(1)}, f32[1,16,128]{2,0,1:T(1,128)S(1)}, u32[]{:S(2)}, u32[]{:S(2)}) collective-permute-start(f32[1,16,128]{2,0,1:T(1,128)S(1)} %get-tuple-element.63), channel_id=1, source_target_pairs={{4,0},{8,4},{12,8},{16,12},{20,16},{24,20},{28,24},{0,28},{5,1},{9... | collective-permute-start | bytes 24584 | tf_op jit(solution)/shard_map/ppermute | solution.py:17
  213.3 1.1 fusion.80
  214.5 0.3 copy.93
  214.8 1.5 collective-permute-done.3
  216.4 0.3 copy.95
  216.6 0.6 collective-permute-done.1
  217.3 1.8 fusion.26
  219.1 1.0 copy.96
  (25 shorter events, 0.4 us)
Async XLA Ops:
  2.1 65.8 %all-to-all-start = ((f32[80,16,128]{2,0,1:T(8,128)}), f32[80,16,128]{2,0,1:T(8,128)S(1)}, u32[]{:S(2)}, u32[]{:S(2)}) async-start(f32[80,16,128]{2,0,1:T(8,128)} %copy.69), calls=%async_computation | async-start | bytes 1310720 | tf_op jit(solution)/shard_map/all_to_all | solution.py:91
  67.9 27.8 %all-to-all-start.1 = ((f32[80,16,128]{2,0,1:T(8,128)}), f32[80,16,128]{2,0,1:T(8,128)}, u32[]{:S(2)}, u32[]{:S(2)}) async-start(f32[80,16,128]{2,0,1:T(8,128)} %copy.77), calls=%async_computation.1 | async-start | bytes 1310720 | tf_op jit(solution)/shard_map/all_to_all | solution.py:90
  84.4 3.5 %copy-start = (s32[640,2,128]{2,0,1:T(8,128)}, s32[640,2,128]{2,0,1:T(8,128)S(1)}, u32[]{:S(2)}) copy-start(s32[640,2,128]{2,0,1:T(8,128)S(1)} %get-tuple-element.49) | copy-start | bytes 1966084
  84.4 8.0 %copy-start.1 = (s32[640,2,128]{2,0,1:T(8,128)}, s32[640,2,128]{2,0,1:T(8,128)S(1)}, u32[]{:S(2)}) copy-start(s32[640,2,128]{2,0,1:T(8,128)S(1)} %get-tuple-element.50) | copy-start | bytes 1966084
  93.6 0.8 copy-start.2
  95.7 50.3 %all-to-all-start.2 = ((f32[80,16,128]{2,0,1:T(8,128)}), f32[80,16,128]{2,0,1:T(8,128)}, u32[]{:S(2)}, u32[]{:S(2)}) async-start(f32[80,16,128]{2,0,1:T(8,128)} %copy.79), calls=%async_computation.2 | async-start | bytes 1310720 | tf_op jit(solution)/shard_map/all_to_all | solution.py:92
  148.9 32.3 %copy-start.3 = (f32[8,80,2,128]{3,1,0,2:T(8,128)S(1)}, f32[8,80,2,128]{3,1,0,2:T(8,128)}, u32[]{:S(2)}) copy-start(f32[8,80,2,128]{3,1,0,2:T(8,128)} %copy.78) | copy-start | bytes 1966084
  183.8 15.2 %all-to-all-start.4 = ((f32[640,2,128]{2,1,0:T(2,128)}), f32[640,2,128]{2,1,0:T(2,128)S(1)}, u32[]{:S(2)}, u32[]{:S(2)}) async-start(f32[640,2,128]{2,1,0:T(2,128)} %copy.86), calls=%async_computation.4 | async-start | bytes 1310720 | tf_op jit(solution)/shard_map/all_to_all | solution.py:99
  199.1 15.3 %all-to-all-start.3 = ((f32[640,2,128]{2,1,0:T(2,128)}), f32[640,2,128]{2,1,0:T(2,128)S(1)}, u32[]{:S(2)}, u32[]{:S(2)}) async-start(f32[640,2,128]{2,1,0:T(2,128)} %copy.83), calls=%async_computation.3 | async-start | bytes 1310720 | tf_op jit(solution)/shard_map/all_to_all | solution.py:98
  207.0 7.5 %collective-permute-start.2 = (f32[80,16,1]{0,1,2:T(8,128)S(1)}, f32[80,16,1]{0,1,2:T(8,128)S(1)}, u32[]{:S(2)}, u32[]{:S(2)}) collective-permute-start(f32[80,16,1]{0,1,2:T(8,128)S(1)} %copy.92), channel_id=1, source_target_pairs={{1,0},{2,1},{3,2},{0,3},{5,4},{6,5},{7,6},{4,7},{9,8},{10,9},{11,1... | collective-permute-start | bytes 15368 | tf_op jit(solution)/shard_map/ppermute | solution.py:17
  210.9 5.5 %collective-permute-start.3 = (f32[80,16,1]{0,1,2:T(8,128)S(1)}, f32[80,16,1]{0,1,2:T(8,128)S(1)}, u32[]{:S(2)}, u32[]{:S(2)}) collective-permute-start(f32[80,16,1]{0,1,2:T(8,128)S(1)} %copy.94), channel_id=1, source_target_pairs={{0,1},{1,2},{2,3},{3,0},{4,5},{5,6},{6,7},{7,4},{8,9},{9,10},{10,1... | collective-permute-start | bytes 15368 | tf_op jit(solution)/shard_map/ppermute | solution.py:14
  210.9 5.7 %collective-permute-start = (f32[1,16,128]{2,0,1:T(1,128)S(1)}, f32[1,16,128]{2,0,1:T(1,128)S(1)}, u32[]{:S(2)}, u32[]{:S(2)}) collective-permute-start(f32[1,16,128]{2,0,1:T(1,128)S(1)} %get-tuple-element.63), channel_id=1, source_target_pairs={{4,0},{8,4},{12,8},{16,12},{20,16},{24,20},{28,24},{0,28},{5,1},{9... | collective-permute-start | bytes 24584 | tf_op jit(solution)/shard_map/ppermute | solution.py:17
  213.3 4.0 %collective-permute-start.1 = (f32[1,16,128]{2,0,1:T(1,128)S(1)}, f32[1,16,128]{2,0,1:T(1,128)S(1)}, u32[]{:S(2)}, u32[]{:S(2)}) collective-permute-start(f32[1,16,128]{2,0,1:T(1,128)S(1)} %get-tuple-element.64), channel_id=1, source_target_pairs={{0,4},{4,8},{8,12},{12,16},{16,20},{20,24},{24,28},{28,0},{1,5},{5... | collective-permute-start | bytes 24584 | tf_op jit(solution)/shard_map/ppermute | solution.py:14
where the time goes:
time: 222 us; the launch traced here: 220 us
  matrix products  76.2 us (34%)
  other arithmetic  49.5 us (22%)
  between operations  32.9 us (15%)
  starting transfers between devices  27.5 us (12%)
  local copies, waits for them, and re-layouts  24.8 us (11%)
  waiting for transfers between devices  9.24 us (4%)
    dot_general x1, matrix products, shards(): jnp.einsum('pckyz,pkx->cxyz', spectra, tables, preferred_element_type=jnp...  32.3 us
    dot_general x1, matrix products, contract(): jnp.einsum('ba,bxyz->axyz', second, upper_hot, precision=lax.Precision.HI...  26.9 us
    dot_general x1, matrix products, contract(): jnp.einsum('ba,bxyz->axyz', second, lower_hot, precision=lax.Precision.HI...  17 us
    add x1, other arithmetic, contract(): upper_hot = (labels == interval[None] + 1).astype(jnp.float32)  12.2 us
    div x1, other arithmetic, spline_second(): lax.linalg.tridiagonal_solve(lower_band, main_band, upper_band, right_side)  10.6 us
    another operation x1, other arithmetic  7.68 us
    unnamed x11, local copies, waits for them, and re-layouts  7.29 us
    all_to_all x1, waiting for transfers between devices, shards(): lax.all_to_all(slab_scale, 'gx', split_axis=0, concat_axis=1, tiled=True)  7.07 us
  transfers between devices with their start and end apart: 9, of which 3 were waited for; matrix products, arithmetic and copies ran while one was open for 49% of the time, Pallas kernels for 0%

commit v1 on v0

--- a/solution.py
+++ b/solution.py
@@ -3,6 +3,18 @@
 import jax.numpy as jnp
 from jax import lax
 from jax.sharding import PartitionSpec as P
+
+
+def exchange_directly(array, axis, split, join):
+    ways, here = (lax.axis_size(axis), lax.axis_index(axis))
+    width = array.shape[split] // ways
+    turned = jnp.roll(array, -here * width, axis=split)
+    got = [lax.slice_in_dim(turned, 0, width, axis=split)]
+    for far in range(1, ways):
+        sent = lax.slice_in_dim(turned, far * width, (far + 1) * width, axis=split)
+        got.append(lax.ppermute(sent, axis, [(d, (d + far) % ways) for d in range(ways)]))
+    line = jnp.concatenate(got[::-1], axis=join)
+    return jnp.roll(line, (here + 1) * got[0].shape[join], axis=join)
 
 
 def extended(block, sides, width):
@@ -96,7 +108,7 @@
     slab_scale = slab_density * sum_slope
     local_term, grad_scale = (
         lax.all_to_all(slab_local, "gx", split_axis=0, concat_axis=1, tiled=True),
-        lax.all_to_all(slab_scale, "gx", split_axis=0, concat_axis=1, tiled=True),
+        exchange_directly(slab_scale, "gx", 0, 1),
     )
     flux_first = grad_scale * wave_gradient[0]
     flux_second = grad_scale * wave_gradient[1]

time: 222 us -> 210 us (0.946)
  waiting for transfers between devices: 9.24 us -> 0.04 us
  starting transfers between devices: 27.5 us -> 32.3 us
  local copies, waits for them, and re-layouts: 24.8 us -> 21.7 us
    dot_general x1, matrix products: 26.9 us -> 17 us  [contract(): jnp.einsum('ba,bxyz->axyz', second, upper_hot, precision=lax.Precision.HI...]
    dot_general x1, matrix products: 17 us -> 26.9 us  [contract(): jnp.einsum('ba,bxyz->axyz', second, lower_hot, precision=lax.Precision.HI...]
    ppermute x0 -> x7, starting transfers between devices: none -> 7.85 us  [exchange_directly(): lax.ppermute(sent, axis, [(d, (d + far) % ways) for d in range(ways)])]
    all_to_all x1 -> x0, waiting for transfers between devices: 7.07 us -> none  [shards(): lax.all_to_all(slab_scale, 'gx', split_axis=0, concat_axis=1, tiled=True)]
    all_to_all x1 -> x0, starting transfers between devices: 4.13 us -> none  [shards(): lax.all_to_all(slab_scale, 'gx', split_axis=0, concat_axis=1, tiled=True)]
    slice x1, local copies, waits for them, and re-layouts: 2.69 us -> 0.05 us  [exchange_directly(): got = [lax.slice_in_dim(turned, 0, width, axis=split)]]
    unnamed x11 -> x25, local copies, waits for them, and re-layouts: 7.29 us -> 7.65 us
  transfers between devices with their start and end apart: 9 -> 15, of which waited for: 3 -> 0; matrix products, arithmetic and copies ran while one was open for 49% -> 51% of each run, Pallas kernels for 0% -> 0%
where the time goes in v1:
time: 210 us; the launch traced here: 209 us
  matrix products  74.1 us (35%)
  other arithmetic  47.8 us (23%)
  between operations  33 us (16%)
  starting transfers between devices  32.3 us (15%)
  local copies, waits for them, and re-layouts  21.7 us (10%)
    dot_general x1, matrix products, shards(): jnp.einsum('pckyz,pkx->cxyz', spectra, tables, preferred_element_type=jnp...  30.2 us
    dot_general x1, matrix products, contract(): jnp.einsum('ba,bxyz->axyz', second, lower_hot, precision=lax.Precision.HI...  26.9 us
    dot_general x1, matrix products, contract(): jnp.einsum('ba,bxyz->axyz', second, upper_hot, precision=lax.Precision.HI...  17 us
    add x1, other arithmetic, contract(): upper_hot = (labels == interval[None] + 1).astype(jnp.float32)  12.2 us
    div x1, other arithmetic, spline_second(): lax.linalg.tridiagonal_solve(lower_band, main_band, upper_band, right_side)  10.7 us
    ppermute x7, starting transfers between devices, exchange_directly(): lax.ppermute(sent, axis, [(d, (d + far) % ways) for d in range(ways)])  7.85 us
    another operation x1, other arithmetic  7.66 us
    unnamed x25, local copies, waits for them, and re-layouts  7.65 us
  transfers between devices with their start and end apart: 15, of which 0 were waited for; matrix products, arithmetic and copies ran while one was open for 51% of the time, Pallas kernels for 0%

profile of v1, /device:TPU:0, one launch (start us, length us, event | category | flops | bytes accessed | tf_op | source)
XLA Modules:
  0.0 208.9 jit_solution(15510656740866985373)
XLA Ops:
  0.0 2.1 %copy.58 = f32[80,16,128]{2,0,1:T(8,128)} copy(f32[80,16,128]{2,1,0:T(8,128)} %param.9) | data formatting | bytes 1310720 | tf_op args[3]
  2.2 5.2 %all-to-all-start = ((f32[80,16,128]{2,0,1:T(8,128)}), f32[80,16,128]{2,0,1:T(8,128)S(1)}, u32[]{:S(2)}, u32[]{:S(2)}) async-start(f32[80,16,128]{2,0,1:T(8,128)} %copy.58), calls=%async_computation | async-start | bytes 1310720 | tf_op jit(solution)/shard_map/all_to_all | solution.py:103
  7.4 0.8 slice_subtract_fusion.19
  8.3 0.7 fusion.81
  9.0 0.7 fusion.82
  40.4 10.7 %fusion.41 = (f32[1,20]{1,0:T(1,128)S(1)}, f32[1,20]{1,0:T(1,128)S(1)}, f32[1,20]{1,0:T(1,128)S(1)}, f32[1,20]{1,0:T(1,128)S(1)}, f32[1,20]{1,0:T(1,128)S(1)}, /...) fusion(f32[18,20]{1,0:T(8,128)S(1)} %fusion.35, ...), kind=kLoop, calls=%fused_computation.98 | loop fusion | flops 980 | bytes 2852 | tf_op jit(solution)/shard_map/eval_jaxpr/div | solution.py:53
  52.5 2.1 %copy.66 = f32[80,16,128]{2,0,1:T(8,128)} copy(f32[80,16,128]{2,1,0:T(8,128)} %param.8) | data formatting | bytes 1310720 | tf_op args[2]
  54.6 2.1 %copy.68 = f32[80,16,128]{2,0,1:T(8,128)} copy(f32[80,16,128]{2,1,0:T(8,128)} %param.10) | data formatting | bytes 1310720 | tf_op args[4]
  57.5 0.7 multiply_subtract_fusion.2
  58.3 2.0 fusion.83
  60.4 7.7 %negate_convert_fusion = (bf16[1,640,640]{1,2,0:T(8,128)(2,1)}, bf16[1,640,640]{1,2,0:T(8,128)(2,1)}) fusion(), kind=kLoop, calls=%fused_computation.21 | loop fusion | flops 4915200 | bytes 1638400 | tf_op jit(solution)/shard_map/convert.1
  68.0 4.2 %all-to-all-start.1 = ((f32[80,16,128]{2,0,1:T(8,128)}), f32[80,16,128]{2,0,1:T(8,128)}, u32[]{:S(2)}, u32[]{:S(2)}) async-start(f32[80,16,128]{2,0,1:T(8,128)} %copy.66), calls=%async_computation.1 | async-start | bytes 1310720 | tf_op jit(solution)/shard_map/all_to_all | solution.py:102
  72.3 12.2 %broadcast_add_fusion = (s32[640,2,128]{2,0,1:T(8,128)S(1)}, s32[640,2,128]{2,0,1:T(8,128)S(1)}) fusion(f32[]{:T(128)} %bitcast.25, f32[]{:T(128)} %bitcast.24, f32[]{:T(128)} %bitcast.23, f32[]{:T(128)} %bitcast.22, f32[]{:T(128)} %bitcast.21, f32[]{:T(128)} %bitcast.20, f32[]{:T(128)} %bitcast.19, f32[]{:T(128)} %bitcast.18, f32[]{:T(128)} %bitcast.17, ...), kind=kLoop, calls=%fused_computation.85 | loop fusion | flops 8847360 | bytes 1966152 | tf_op jit(solution)/shard_map/add | solution.py:80
  84.6 4.4 %iota_compare_fusion = (pred[20,640,2,128]{3,1,2,0:T(32,128)(4,1)}, pred[20,640,2,128]{3,1,2,0:T(32,128)(4,1)S(1)}) fusion(s32[640,2,128]{2,0,1:T(8,128)S(1)} %get-tuple-element.49, s32[640,2,128]{2,0,1:T(8,128)S(1)} %get-tuple-element.50), kind=kLoop, calls=%fused_computation.13 | loop fusion | flops 6553600 | bytes 7864320 | tf_op jit(solution)/shard_map/eq | solution.py:80
  89.0 2.7 %select_reduce_fusion = (f32[640,2,128]{2,0,1:T(8,128)S(1)}, f32[640,2,128]{2,0,1:T(8,128)S(1)}) fusion(f32[20]{0:T(128)S(1)} %copy-done.6, s32[640,2,128]{2,0,1:T(8,128)S(1)} %get-tuple-element.50, s32[640,2,128]{2,0,1:T(8,128)S(1)} %get-tuple-element.49), kind=kLoop, calls=%fused_computation.11 | loop fusion | flops 19333120 | bytes 2621520 | tf_op jit(solution)/shard_map/reduce_sum | solution.py:82
  91.6 1.1 fusion.15
  92.7 1.5 fusion.16
  94.2 0.8 copy-done.3
  95.0 1.0 fusion.22
  96.0 4.4 %all-to-all-start.2 = ((f32[80,16,128]{2,0,1:T(8,128)}), f32[80,16,128]{2,0,1:T(8,128)}, u32[]{:S(2)}, u32[]{:S(2)}) async-start(f32[80,16,128]{2,0,1:T(8,128)} %copy.68), calls=%async_computation.2 | async-start | bytes 1310720 | tf_op jit(solution)/shard_map/all_to_all | solution.py:104
  100.4 2.0 copy.67
  102.4 17.0 %fusion = f32[20,640,2,128]{3,0,2,1:T(8,128)} fusion(pred[20,640,2,128]{3,1,2,0:T(32,128)(4,1)} %get-tuple-element.129, f32[20,20]{1,0:T(8,128)S(1)} %concatenate.36), kind=kOutput, calls=%fused_computation | convolution fusion | flops 786432000 | bytes 16385600 | tf_op jit(solution)/shard_map/ba,bxyz->axyz/dot_general | solution.py:88
  119.4 26.9 %fusion.2 = f32[20,640,2,128]{3,0,2,1:T(8,128)} fusion(pred[20,640,2,128]{3,1,2,0:T(32,128)(4,1)S(1)} %get-tuple-element.130, f32[20,20]{1,0:T(8,128)S(1)} %concatenate.36), kind=kOutput, calls=%fused_computation.2 | convolution fusion | flops 786432000 | bytes 16385600 | tf_op jit(solution)/shard_map/ba,bxyz->axyz/dot_general | solution.py:87
  146.3 1.1 copy.69
  147.4 30.2 %fusion.5 = (f32[640,2,128]{2,0,1:T(8,128)S(1)}, f32[640,2,128]{2,0,1:T(8,128)S(1)}) fusion(f32[20,640,2,128]{3,0,2,1:T(8,128)} %fusion, f32[20,640,2,128]{3,0,2,1:T(8,128)} %fusion.2, f32[640,2,128]{2,0,1:T(8,128)} %fusion.22, f32[640,2,128]{2,0,1:T(8,128)} %get-tuple-element.72, f32[640,2,128]{2,0,1:T(8,128)} %copy-done.2, s32[640,2,128]{2,0,1:T(8,128)} %copy-done, ...), kind=kOutput, calls=%fused_computation.7 | convolution fusion | flops 8463646720 | bytes 48168960 | tf_op jit(solution)/shard_map/pckyz,pkx->cxyz/dot_general | solution.py:98
  177.6 0.2 bitcast_multiply_fusion.7
  177.8 0.2 fusion.23
  178.2 2.7 %collective-permute-start = (f32[80,2,128]{2,1,0:T(2,128)S(1)}, f32[80,2,128]{2,1,0:T(2,128)S(1)}, u32[]{:S(2)}, u32[]{:S(2)}) collective-permute-start(f32[80,2,128]{2,1,0:T(2,128)S(1)} %copy.86), channel_id=1, source_target_pairs={{0,28},{4,0},{8,4},{12,8},{16,12},{20,16},{24,20},{28,24},{1,29},{... | collective-permute-start | bytes 245768 | tf_op jit(solution)/shard_map/ppermute | solution.py:15
  180.9 0.6 collective-permute-start.1
  181.5 0.2 collective-permute-start.2
  181.7 1.5 collective-permute-start.3
  183.3 0.3 collective-permute-start.4
  183.7 2.6 %collective-permute-start.5 = (f32[80,2,128]{2,1,0:T(2,128)S(1)}, f32[80,2,128]{2,1,0:T(2,128)S(1)}, u32[]{:S(2)}, u32[]{:S(2)}) collective-permute-start(f32[80,2,128]{2,1,0:T(2,128)S(1)} %copy.91), channel_id=1, source_target_pairs={{0,8},{4,12},{8,16},{12,20},{16,24},{20,28},{24,0},{28,4},{1,9},{5... | collective-permute-start | bytes 245768 | tf_op jit(solution)/shard_map/ppermute | solution.py:15
  186.3 1.3 copy.72
  187.7 4.2 %all-to-all-start.3 = ((f32[640,2,128]{2,1,0:T(2,128)}), f32[640,2,128]{2,1,0:T(2,128)}, u32[]{:S(2)}, u32[]{:S(2)}) async-start(f32[640,2,128]{2,1,0:T(2,128)} %copy.72), calls=%async_computation.3 | async-start | bytes 1310720 | tf_op jit(solution)/shard_map/all_to_all | solution.py:110
  192.0 1.3 concatenate.38
  193.3 1.7 bitcast_multiply_fusion.5
  195.0 0.2 fusion.79
  195.2 0.3 copy.77
  195.5 1.6 collective-permute-start.10
  197.1 0.3 copy.75
  197.4 2.2 %collective-permute-start.9 = (f32[80,16,1]{0,1,2:T(8,128)S(1)}, f32[80,16,1]{0,1,2:T(8,128)S(1)}, u32[]{:S(2)}, u32[]{:S(2)}) collective-permute-start(f32[80,16,1]{0,1,2:T(8,128)S(1)} %copy.75), channel_id=1, source_target_pairs={{1,0},{2,1},{3,2},{0,3},{5,4},{6,5},{7,6},{4,7},{9,8},{10,9},{11,1... | collective-permute-start | bytes 15368 | tf_op jit(solution)/shard_map/ppermute | solution.py:29
  199.7 0.3 collective-permute-start.8
  199.9 2.4 %collective-permute-start.7 = (f32[1,16,128]{2,1,0:T(8,128)S(1)}, f32[1,16,128]{2,1,0:T(8,128)S(1)}, u32[]{:S(2)}, u32[]{:S(2)}) collective-permute-start(f32[1,16,128]{2,1,0:T(8,128)S(1)} %get-tuple-element.60), channel_id=1, source_target_pairs={{4,0},{8,4},{12,8},{16,12},{20,16},{24,20},{28,24},{0,28},{5,1},{9... | collective-permute-start | bytes 24584 | tf_op jit(solution)/shard_map/ppermute | solution.py:29
  202.5 1.2 copy.78
  203.7 1.1 copy.76
  204.8 1.3 copy.73
  206.2 2.7 %fusion.27 = f32[80,16,128]{2,1,0:T(8,128)} fusion(f32[80,16,128]{2,1,0:T(8,128)S(1)} %bitcast.173, f32[80,16,128]{2,1,0:T(8,128)S(1)} %get-tuple-element.53, f32[80,16,1]{2,1,0:T(8,128)} %copy.78, f32[80,16,1]{2,1,0:T(8,128)} %copy.76, f32[80,16,128]{2,1,0:T(8,128)S(1)} %get-tuple-element.52, f32[1,16,128]{2,1,0:T(8,128)S(1)} %collective-permute-done.8, ...), kind=kLoop, calls=%fused_computation.48 | loop fusion | flops 2129920 | bytes 3958784 | tf_op jit(solution)/shard_map/sub | solution.py:121
  (48 shorter events, 1.0 us)
Async XLA Ops:
  0.0 89.0 %copy-start.6 = (f32[20]{0:T(128)S(1)}, f32[20]{0:T(128)}, u32[]{:S(2)}) copy-start(f32[20]{0:T(128)} %param.7) | copy-start | bytes 244
  2.2 65.9 %all-to-all-start = ((f32[80,16,128]{2,0,1:T(8,128)}), f32[80,16,128]{2,0,1:T(8,128)S(1)}, u32[]{:S(2)}, u32[]{:S(2)}) async-start(f32[80,16,128]{2,0,1:T(8,128)} %copy.58), calls=%async_computation | async-start | bytes 1310720 | tf_op jit(solution)/shard_map/all_to_all | solution.py:103
  68.0 28.0 %all-to-all-start.1 = ((f32[80,16,128]{2,0,1:T(8,128)}), f32[80,16,128]{2,0,1:T(8,128)}, u32[]{:S(2)}, u32[]{:S(2)}) async-start(f32[80,16,128]{2,0,1:T(8,128)} %copy.66), calls=%async_computation.1 | async-start | bytes 1310720 | tf_op jit(solution)/shard_map/all_to_all | solution.py:102
  84.5 9.7 %copy-start = (s32[640,2,128]{2,0,1:T(8,128)}, s32[640,2,128]{2,0,1:T(8,128)S(1)}, u32[]{:S(2)}) copy-start(s32[640,2,128]{2,0,1:T(8,128)S(1)} %get-tuple-element.49) | copy-start | bytes 1966084
  84.5 9.6 %copy-start.1 = (s32[640,2,128]{2,0,1:T(8,128)}, s32[640,2,128]{2,0,1:T(8,128)S(1)}, u32[]{:S(2)}) copy-start(s32[640,2,128]{2,0,1:T(8,128)S(1)} %get-tuple-element.50) | copy-start | bytes 1966084
  92.7 1.5 copy-start.2
  92.7 1.5 copy-start.4
  94.2 0.9 copy-start.3
  96.0 50.3 %all-to-all-start.2 = ((f32[80,16,128]{2,0,1:T(8,128)}), f32[80,16,128]{2,0,1:T(8,128)}, u32[]{:S(2)}, u32[]{:S(2)}) async-start(f32[80,16,128]{2,0,1:T(8,128)} %copy.68), calls=%async_computation.2 | async-start | bytes 1310720 | tf_op jit(solution)/shard_map/all_to_all | solution.py:104
  147.4 30.2 %copy-start.5 = (f32[80,8,2,128]{3,0,1,2:T(8,128)S(1)}, f32[80,8,2,128]{3,0,1,2:T(8,128)}, u32[]{:S(2)}) copy-start(f32[80,8,2,128]{3,0,1,2:T(8,128)} %copy.67) | copy-start | bytes 1966084
  178.2 5.6 %collective-permute-start = (f32[80,2,128]{2,1,0:T(2,128)S(1)}, f32[80,2,128]{2,1,0:T(2,128)S(1)}, u32[]{:S(2)}, u32[]{:S(2)}) collective-permute-start(f32[80,2,128]{2,1,0:T(2,128)S(1)} %copy.86), channel_id=1, source_target_pairs={{0,28},{4,0},{8,4},{12,8},{16,12},{20,16},{24,20},{28,24},{1,29},{... | collective-permute-start | bytes 245768 | tf_op jit(solution)/shard_map/ppermute | solution.py:15
  180.9 5.4 %collective-permute-start.1 = (f32[80,2,128]{2,1,0:T(2,128)S(1)}, f32[80,2,128]{2,1,0:T(2,128)S(1)}, u32[]{:S(2)}, u32[]{:S(2)}) collective-permute-start(f32[80,2,128]{2,1,0:T(2,128)S(1)} %copy.87), channel_id=1, source_target_pairs={{0,24},{4,28},{8,0},{12,4},{16,8},{20,12},{24,16},{28,20},{1,25},{... | collective-permute-start | bytes 245768 | tf_op jit(solution)/shard_map/ppermute | solution.py:15
  181.5 10.4 %collective-permute-start.2 = (f32[80,2,128]{2,1,0:T(2,128)S(1)}, f32[80,2,128]{2,1,0:T(2,128)S(1)}, u32[]{:S(2)}, u32[]{:S(2)}) collective-permute-start(f32[80,2,128]{2,1,0:T(2,128)S(1)} %copy.88), channel_id=1, source_target_pairs={{0,20},{4,24},{8,28},{12,0},{16,4},{20,8},{24,12},{28,16},{1,21},{... | collective-permute-start | bytes 245768 | tf_op jit(solution)/shard_map/ppermute | solution.py:15
  181.7 10.2 %collective-permute-start.3 = (f32[80,2,128]{2,1,0:T(2,128)S(1)}, f32[80,2,128]{2,1,0:T(2,128)S(1)}, u32[]{:S(2)}, u32[]{:S(2)}) collective-permute-start(f32[80,2,128]{2,1,0:T(2,128)S(1)} %copy.89), channel_id=1, source_target_pairs={{0,16},{4,20},{8,24},{12,28},{16,0},{20,4},{24,8},{28,12},{1,17},{... | collective-permute-start | bytes 245768 | tf_op jit(solution)/shard_map/ppermute | solution.py:15
  183.3 8.7 %collective-permute-start.4 = (f32[80,2,128]{2,1,0:T(2,128)S(1)}, f32[80,2,128]{2,1,0:T(2,128)S(1)}, u32[]{:S(2)}, u32[]{:S(2)}) collective-permute-start(f32[80,2,128]{2,1,0:T(2,128)S(1)} %copy.90), channel_id=1, source_target_pairs={{0,12},{4,16},{8,20},{12,24},{16,28},{20,0},{24,4},{28,8},{1,13},{... | collective-permute-start | bytes 245768 | tf_op jit(solution)/shard_map/ppermute | solution.py:15
  183.7 8.2 %collective-permute-start.5 = (f32[80,2,128]{2,1,0:T(2,128)S(1)}, f32[80,2,128]{2,1,0:T(2,128)S(1)}, u32[]{:S(2)}, u32[]{:S(2)}) collective-permute-start(f32[80,2,128]{2,1,0:T(2,128)S(1)} %copy.91), channel_id=1, source_target_pairs={{0,8},{4,12},{8,16},{12,20},{16,24},{20,28},{24,0},{28,4},{1,9},{5... | collective-permute-start | bytes 245768 | tf_op jit(solution)/shard_map/ppermute | solution.py:15
  186.3 5.6 %collective-permute-start.6 = (f32[80,2,128]{2,1,0:T(2,128)S(1)}, f32[80,2,128]{2,1,0:T(2,128)S(1)}, u32[]{:S(2)}, u32[]{:S(2)}) collective-permute-start(f32[80,2,128]{2,1,0:T(2,128)S(1)} %copy.92), channel_id=1, source_target_pairs={{0,4},{4,8},{8,12},{12,16},{16,20},{20,24},{24,28},{28,0},{1,5},{5... | collective-permute-start | bytes 245768 | tf_op jit(solution)/shard_map/ppermute | solution.py:15
  187.7 17.2 %all-to-all-start.3 = ((f32[640,2,128]{2,1,0:T(2,128)}), f32[640,2,128]{2,1,0:T(2,128)}, u32[]{:S(2)}, u32[]{:S(2)}) async-start(f32[640,2,128]{2,1,0:T(2,128)} %copy.72), calls=%async_computation.3 | async-start | bytes 1310720 | tf_op jit(solution)/shard_map/all_to_all | solution.py:110
  195.5 7.0 %collective-permute-start.10 = (f32[80,16,1]{0,1,2:T(8,128)S(1)}, f32[80,16,1]{0,1,2:T(8,128)S(1)}, u32[]{:S(2)}, u32[]{:S(2)}) collective-permute-start(f32[80,16,1]{0,1,2:T(8,128)S(1)} %copy.77), channel_id=1, source_target_pairs={{0,1},{1,2},{2,3},{3,0},{4,5},{5,6},{6,7},{7,4},{8,9},{9,10},{10,1... | collective-permute-start | bytes 15368 | tf_op jit(solution)/shard_map/ppermute | solution.py:26
  197.4 6.3 %collective-permute-start.9 = (f32[80,16,1]{0,1,2:T(8,128)S(1)}, f32[80,16,1]{0,1,2:T(8,128)S(1)}, u32[]{:S(2)}, u32[]{:S(2)}) collective-permute-start(f32[80,16,1]{0,1,2:T(8,128)S(1)} %copy.75), channel_id=1, source_target_pairs={{1,0},{2,1},{3,2},{0,3},{5,4},{6,5},{7,6},{4,7},{9,8},{10,9},{11,1... | collective-permute-start | bytes 15368 | tf_op jit(solution)/shard_map/ppermute | solution.py:29
  199.7 6.5 %collective-permute-start.8 = (f32[1,16,128]{2,1,0:T(8,128)S(1)}, f32[1,16,128]{2,1,0:T(8,128)S(1)}, u32[]{:S(2)}, u32[]{:S(2)}) collective-permute-start(f32[1,16,128]{2,1,0:T(8,128)S(1)} %get-tuple-element.61), channel_id=1, source_target_pairs={{0,4},{4,8},{8,12},{12,16},{16,20},{20,24},{24,28},{28,0},{1,5},{5... | collective-permute-start | bytes 24584 | tf_op jit(solution)/shard_map/ppermute | solution.py:26
  199.9 6.2 %collective-permute-start.7 = (f32[1,16,128]{2,1,0:T(8,128)S(1)}, f32[1,16,128]{2,1,0:T(8,128)S(1)}, u32[]{:S(2)}, u32[]{:S(2)}) collective-permute-start(f32[1,16,128]{2,1,0:T(8,128)S(1)} %get-tuple-element.60), channel_id=1, source_target_pairs={{4,0},{8,4},{12,8},{16,12},{20,16},{24,20},{28,24},{0,28},{5,1},{9... | collective-permute-start | bytes 24584 | tf_op jit(solution)/shard_map/ppermute | solution.py:29
